TPU v7x, 8 devices: a whole 2x2x1 slice. The times are simulated.
8 devices in a mesh: dp: 1 (over z), ep: 8 (over x, y, core).
Axes of the slice: x: 2, y: 2, z: 1, core: 2. Of those that a mesh axis runs over, the one named last changes fastest.
Arguments:
- x: bfloat16 [1, 8, 256, 2048], P('dp', 'ep')
- expert: int32 [1, 8, 256, 8], P('dp', 'ep')
- slot: int32 [1, 8, 256, 8], P('dp', 'ep')
- gate: float32 [1, 8, 256, 8], P('dp', 'ep')
- w_gate: bfloat16 [64, 2048, 1024], P('ep')
- w_up: bfloat16 [64, 2048, 1024], P('ep')
- w_down: bfloat16 [64, 1024, 2048], P('ep')
Outputs:
- y: bfloat16 [1, 8, 256, 2048], P('dp', 'ep')
All inputs are finite; a program needn't handle non-finite values.
Results may differ from a plain program's by a relative error of at most 0.009.
Values are sent between devices in bfloat16 or wider.
A program may use at most 2 GiB of HBM per device.

v0:
```python
import jax
import jax.numpy as jnp
from jax import lax
from jax.sharding import NamedSharding, PartitionSpec as P


def einsum(form, a, b):
    return jnp.einsum(form, a.astype(jnp.float32), b.astype(jnp.float32))


def solution(mesh):
    def placed(v, *spec):
        return lax.with_sharding_constraint(v, NamedSharding(mesh, P(*spec)))

    def step(x, expert, slot, gate, w_gate, w_up, w_down):
        experts, (tokens, top) = w_gate.shape[0], expert.shape[2:]
        slots = 5 * tokens * top // (4 * experts)
        to_expert = jax.nn.one_hot(expert, experts, dtype=jnp.bfloat16)
        to_slot = jax.nn.one_hot(slot, slots, dtype=jnp.bfloat16)
        weighted = to_expert * gate[..., None].astype(jnp.bfloat16)
        dispatch = einsum("abtke,abtkc->abtec", to_expert, to_slot).astype(jnp.bfloat16)
        combine = einsum("abtke,abtkc->abtec", weighted, to_slot).astype(jnp.bfloat16)
        z = einsum("abtec,abtd->aebcd", dispatch, x).astype(jnp.bfloat16)
        z = placed(z, "dp", None, "ep", None, None)
        z = placed(z, "dp", "ep", None, None, None)
        h = jax.nn.silu(einsum("aebcd,edf->aebcf", z, w_gate))
        h = (h * einsum("aebcd,edf->aebcf", z, w_up)).astype(jnp.bfloat16)
        out = einsum("aebcf,efd->aebcd", h, w_down).astype(jnp.bfloat16)
        out = placed(out, "dp", "ep", None, None, None)
        out = placed(out, "dp", None, "ep", None, None)
        y = einsum("abtec,aebcd->abtd", combine, out)
        return y.astype(jnp.bfloat16)

    return step
```

profile of v0, /device:TPU:0, one launch (start us, length us, event | category | flops | bytes accessed | tf_op | source)
XLA Modules:
  0.0 337.1 jit_solution(11158384729813127030)
XLA Ops:
  0.0 0.0 copy-start
  0.0 0.9 copy.10
  0.9 0.8 copy.12
  1.7 3.6 %convolution_convert_fusion.1 = bf16[256,64,40]{1,2,0:T(8,128)(2,1)} fusion(s32[256,8]{1,0:T(8,128)S(1)} %copy.12, s32[256,8]{1,0:T(8,128)S(1)} %copy.10), kind=kOutput, calls=%fused_computation.23 | convolution fusion | flops 11354112 | bytes 1327104 | tf_op jit(solution)/abtke,abtkc->abtec/dot_general | solution.py:8
  5.4 5.6 %copy.13 = bf16[256,64,40]{0,2,1:T(8,128)(2,1)S(1)} copy(bf16[256,64,40]{1,2,0:T(8,128)(2,1)} %convolution_convert_fusion.1) | data formatting | bytes 2621440 | tf_op jit(solution)/convert_element_type | solution.py:21
  11.0 0.0 copy-done
  11.0 3.1 convolution_convert_fusion
  14.1 119.9 %all-to-all.4 = bf16[1,8,8,1,40,2048]{5,4,2,3,0,1:T(8,128)(2,1)} all-to-all(bf16[1,8,8,1,40,2048]{5,4,2,3,0,1:T(8,128)(2,1)S(1)} %bitcast.110), channel_id=1, replica_groups=mesh['dp'=1,'ep'=8] {'ep'}, dimensions={1} | all-to-all | bytes 20971520 | tf_op jit(solution)/sharding_constraint;jit(solution)/sharding_constraint | solution.py:13
  134.0 22.0 %fusion.2 = f32[8,8,40,1024]{3,2,1,0:T(8,128)} fusion(bf16[8,2048,1024]{2,1,0:T(8,128)(2,1)} %param.5, bf16[1,8,8,1,40,2048]{5,4,2,3,0,1:T(8,128)(2,1)} %all-to-all.4), kind=kOutput, calls=%fused_computation.2 | convolution fusion | flops 10737418240 | bytes 54525952 | tf_op jit(solution)/aebcd,edf->aebcf/dot_general | solution.py:8
  156.0 23.2 %fusion.6 = bf16[1,8,8,40,1024]{4,3,2,1,0:T(8,128)(2,1)} fusion(f32[8,8,40,1024]{3,2,1,0:T(8,128)} %fusion.2, bf16[8,2048,1024]{2,1,0:T(8,128)(2,1)} %param.4, bf16[1,8,8,1,40,2048]{5,4,2,3,0,1:T(8,128)(2,1)} %all-to-all.4), kind=kOutput, calls=%fused_computation.7 | convolution fusion | flops 10753146880 | bytes 59768832 | tf_op jit(solution)/aebcd,edf->aebcf/dot_general | solution.py:8
  179.3 20.5 %convert_bitcast_fusion = bf16[1,8,8,1,40,2048]{5,4,2,1,3,0:T(8,128)(2,1)} fusion(bf16[8,1024,2048]{2,1,0:T(8,128)(2,1)} %param.6, bf16[1,8,8,40,1024]{4,3,2,1,0:T(8,128)(2,1)} %fusion.6), kind=kOutput, calls=%fused_computation.15 | convolution fusion | flops 10742661120 | bytes 49283072 | tf_op jit(solution)/aebcf,efd->aebcd/dot_general | solution.py:8
  199.7 10.1 %copy.16 = bf16[1,8,8,1,40,2048]{5,4,1,3,0,2:T(8,128)(2,1)} copy(bf16[1,8,8,1,40,2048]{5,4,2,1,3,0:T(8,128)(2,1)} %convert_bitcast_fusion) | data formatting | bytes 20971520 | tf_op jit(solution)/sharding_constraint;jit(solution)/sharding_constraint | solution.py:13
  209.9 0.0 copy-start.2
  209.9 4.2 %all-to-all-start.1 = ((bf16[1,8,8,1,40,2048]{5,4,1,3,0,2:T(8,128)(2,1)}), bf16[1,8,8,1,40,2048]{5,4,1,3,0,2:T(8,128)(2,1)}, u32[]{:S(2)}, u32[]{:S(2)}) async-start(bf16[1,8,8,1,40,2048]{5,4,1,3,0,2:T(8,128)(2,1)} %copy.16), calls=%async_computation.1 | async-start | bytes 20971520 | tf_op jit(solution)/sharding_constraint;jit(solution)/sharding_constraint | solution.py:13
  214.1 0.0 copy-done.2
  214.2 0.1 copy.11
  214.3 0.0 copy-start.1
  214.3 4.3 %convolution_convert_fusion.2 = bf16[256,64,40]{1,2,0:T(8,128)(2,1)} fusion(s32[256,8]{1,0:T(8,128)S(1)} %copy.12, s32[256,8]{1,0:T(8,128)S(1)} %copy.10, bf16[256,8]{1,0:T(8,128)(2,1)S(1)} %copy.11), kind=kOutput, calls=%fused_computation.24 | convolution fusion | flops 11485184 | bytes 1331200 | tf_op jit(solution)/abtke,abtkc->abtec/dot_general | solution.py:8
  218.6 5.6 %copy.23 = bf16[256,64,40]{0,2,1:T(8,128)(2,1)S(1)} copy(bf16[256,64,40]{1,2,0:T(8,128)(2,1)} %convolution_convert_fusion.2) | data formatting | bytes 2621440 | tf_op jit(solution)/convert_element_type | solution.py:22
  224.2 105.0 %all-to-all-done.1 = bf16[1,8,8,1,40,2048]{5,4,1,3,0,2:T(8,128)(2,1)} async-done(((bf16[1,8,8,1,40,2048]{5,4,1,3,0,2:T(8,128)(2,1)}), bf16[1,8,8,1,40,2048]{5,4,1,3,0,2:T(8,128)(2,1)}, u32[]{:S(2)}, u32[]{:S(2)}) %all-to-all-start.1) | async-done | bytes 10485792 | tf_op jit(solution)/sharding_constraint;jit(solution)/sharding_constraint | solution.py:13
  329.2 7.8 %fusion.22 = bf16[1,1,256,2048]{3,2,1,0:T(8,128)(2,1)} fusion(bf16[256,64,40]{0,2,1:T(8,128)(2,1)S(1)} %copy.23, bf16[64,40,2048]{2,1,0:T(8,128)(2,1)} %bitcast.38), kind=kOutput, calls=%fused_computation.22 | convolution fusion | flops 2684878848 | bytes 12845056 | tf_op jit(solution)/abtec,aebcd->abtd/dot_general | solution.py:8
  337.1 0.0 copy-done.1
  (1 shorter events, 0.0 us)
Async XLA Ops:
  0.0 11.0 %copy-start = (bf16[1,1,256,2048]{3,2,1,0:T(8,128)(2,1)S(1)}, bf16[1,1,256,2048]{3,2,1,0:T(8,128)(2,1)}, u32[]{:S(2)}) copy-start(bf16[1,1,256,2048]{3,2,1,0:T(8,128)(2,1)} %param.3) | copy-start | bytes 3145732
  209.9 4.2 %copy-start.2 = (f32[1,1,256,8]{2,3,1,0:T(8,128)S(1)}, f32[1,1,256,8]{2,3,1,0:T(8,128)}, u32[]{:S(2)}) copy-start(f32[1,1,256,8]{2,3,1,0:T(8,128)} %param.1) | copy-start | bytes 24580
  209.9 119.3 %all-to-all-start.1 = ((bf16[1,8,8,1,40,2048]{5,4,1,3,0,2:T(8,128)(2,1)}), bf16[1,8,8,1,40,2048]{5,4,1,3,0,2:T(8,128)(2,1)}, u32[]{:S(2)}, u32[]{:S(2)}) async-start(bf16[1,8,8,1,40,2048]{5,4,1,3,0,2:T(8,128)(2,1)} %copy.16), calls=%async_computation.1 | async-start | bytes 20971520 | tf_op jit(solution)/sharding_constraint;jit(solution)/sharding_constraint | solution.py:13
  214.3 122.8 %copy-start.1 = (bf16[1,1,256,2048]{3,2,1,0:T(8,128)(2,1)S(1)}, bf16[1,1,256,2048]{3,2,1,0:T(8,128)(2,1)}, u32[]{:S(2)}) copy-start(bf16[1,1,256,2048]{3,2,1,0:T(8,128)(2,1)} %param.3) | copy-start | bytes 3145732
where the time goes:
time: 338 us; the launch traced here: 337 us
  blocking collectives  120 us (36%)
  waiting for transfers between devices  105 us (31%)
  matrix products  84.6 us (25%)
  local copies, waits for them, and re-layouts  23.2 us (7%)
  starting transfers between devices  4.23 us (1%)
    another operation x1, blocking collectives, placed(): return lax.with_sharding_constraint(v, NamedSharding(mesh, P(*spec)))  120 us
    another operation x1, waiting for transfers between devices, placed(): return lax.with_sharding_constraint(v, NamedSharding(mesh, P(*spec)))  105 us
    dot_general x7, matrix products, einsum(): return jnp.einsum(form, a.astype(jnp.float32), b.astype(jnp.float32))  84.6 us
    another operation x1, local copies, waits for them, and re-layouts, placed(): return lax.with_sharding_constraint(v, NamedSharding(mesh, P(*spec)))  10.1 us
  transfers between devices with their start and end apart: 1, of which 1 were waited for; matrix products, arithmetic and copies ran while one was open for 3% of the time, Pallas kernels for 0%

commit v1 on v0

v1 whole, which is shorter than its diff:
```python
import functools

import jax
import jax.numpy as jnp
from jax import lax
from jax.experimental import pallas as pl
from jax.experimental.pallas import tpu as pltpu
from jax.sharding import PartitionSpec as P

MESH = pl.DeviceIdType.MESH
F32, BF16 = jnp.float32, jnp.bfloat16

CORE, Y, X = 1, 2, 4
WR, DR = 6, 8
LAG = 3


def kernel(
    cfg, meta_ref, x_ref, wg_ref, wu_ref, wd_ref, o_ref,
    meta, xall, acc, hid, z, wring, dring, disp, comb, outb,
    part, psend, prec, keep, s1x, s1y, r1x, r1y, s2x, s2y, r2x, r2y,
    meta_ss, meta_rs, load_s, ag_ss, ag_rs, wsem, dsem, p_ss, p_rs, h1_ss, h1_rs, h2_ss, h2_rs,
):
    tokens, d, ff, experts, slots, kc, nc = cfg
    rows = experts * slots
    kn, nn = d // kc, d // nc
    half = tokens // 2
    wide = 2 * slots
    dp, me = lax.axis_index("dp"), lax.axis_index("ep")

    def dev(mask):
        to = me
        for bit in (CORE, Y, X):
            if mask & bit:
                to = to + bit - 2 * bit * ((me // bit) % 2)
        return (dp, to)

    def remote(src, dst, ss, rs, mask):
        return pltpu.make_async_remote_copy(
            src_ref=src, dst_ref=dst, send_sem=ss, recv_sem=rs, device_id=dev(mask), device_id_type=MESH
        )

    def w_copies(i):
        e, k, slot = i % experts, i // experts, i % WR
        at = pl.ds(pl.multiple_of(k * kc, kc), kc)
        return (
            pltpu.make_async_copy(wg_ref.at[e, at], wring.at[slot, 0], wsem.at[slot, 0]),
            pltpu.make_async_copy(wu_ref.at[e, at], wring.at[slot, 1], wsem.at[slot, 1]),
        )

    def d_copy(i):
        e, n, slot = i % experts, i // experts, i % DR
        at = pl.ds(pl.multiple_of(n * nc, nc), nc)
        return pltpu.make_async_copy(wd_ref.at[e, :, at], dring.at[slot], dsem.at[slot])

    def to_x(k):
        return remote(xall.at[0, k], xall.at[X, k], ag_ss.at[0, k], ag_rs.at[0, k], X)

    def to_y(k):
        return remote(xall.at[0, k], xall.at[Y, k], ag_ss.at[1, k], ag_rs.at[1, k], Y)

    def to_core(k):
        return remote(xall.at[0, k], xall.at[CORE, k], ag_ss.at[2, k], ag_rs.at[2, k], CORE)

    def x_to_core(k):
        return remote(xall.at[X, k], xall.at[X | CORE, k], ag_ss.at[3, k], ag_rs.at[3, k], CORE)

    def y_to_core(k):
        return remote(xall.at[Y, k], xall.at[Y | CORE, k], ag_ss.at[4, k], ag_rs.at[4, k], CORE)

    def x_to_y(k):
        at = pl.ds(0, half)
        return remote(xall.at[X, k, at], xall.at[X | Y, k, at], ag_ss.at[5, k], ag_rs.at[5, k], Y)

    def y_to_x(k):
        at = pl.ds(half, half)
        return remote(xall.at[Y, k, at], xall.at[X | Y, k, at], ag_ss.at[6, k], ag_rs.at[6, k], X)

    def xy_to_core(k):
        return remote(xall.at[X | Y, k], xall.at[7, k], ag_ss.at[7, k], ag_rs.at[7, k], CORE)

    exchange = (to_x, to_y, to_core, x_to_core, y_to_core, x_to_y, y_to_x, xy_to_core)

    def own(k):
        at = pl.ds(pl.multiple_of(k * kc, kc), kc)
        return pltpu.make_async_copy(x_ref.at[:, at], xall.at[0, k], load_s.at[k])

    for k in range(kn):
        own(k).start()
    load_meta = pltpu.make_async_copy(meta_ref, meta.at[0], load_s.at[kn])
    load_meta.start()
    for i in range(WR):
        for copy in w_copies(i):
            copy.start()

    barrier = pltpu.get_barrier_semaphore()
    for mask in range(1, 8):
        pl.semaphore_signal(barrier, inc=1, device_id=dev(mask), device_id_type=MESH)
    load_meta.wait()
    pl.semaphore_wait(barrier, 7)

    metas = [
        remote(meta.at[0], meta.at[mask], meta_ss.at[mask], meta_rs.at[mask], mask) for mask in range(1, 8)
    ]
    for copy in metas:
        copy.start()

    def first_hop(k):
        own(k).wait()
        to_x(k).start()
        to_y(k).start()
        to_core(k).start()

    first_hop(0)
    first_hop(1)

    def clear(e, _):
        acc[e] = jnp.zeros(acc.shape[1:], F32)
        return 0

    lax.fori_loop(0, experts, clear, 0)

    for copy in metas:
        copy.wait()

    def tables(r, _):
        row = lax.broadcasted_iota(jnp.int32, (rows, tokens), 0).astype(F32)
        at = meta[r]
        code = at[:8] - (me * rows).astype(F32)
        gate = at[8:]
        hit = jnp.zeros((rows, tokens), F32)
        weight = jnp.zeros((rows, tokens), F32)
        for j in range(8):
            same = code[j : j + 1] == row
            hit = jnp.where(same, 1.0, hit)
            weight = jnp.where(same, gate[j : j + 1], weight)
        disp[r] = hit.astype(BF16)
        comb[r] = jnp.transpose(weight).astype(BF16)
        return 0

    lax.fori_loop(0, 8, tables, 0)

    def project(k):
        for pair in range(4):
            z0 = jnp.dot(disp[2 * pair], xall[2 * pair, k], preferred_element_type=F32)
            z1 = jnp.dot(disp[2 * pair + 1], xall[2 * pair + 1, k], preferred_element_type=F32)
            both = jnp.concatenate(
                [z0.reshape(experts, slots, kc), z1.reshape(experts, slots, kc)], axis=1
            ).astype(BF16)
            z[:, pair * wide : (pair + 1) * wide, :] = both

        def one(e, _):
            i = k * experts + e
            slot = i % WR
            for copy in w_copies(i):
                copy.wait()
            lhs = z[e]
            step = 512
            for part_ in range(2):
                for c in range(0, ff, step):
                    got = jnp.dot(lhs, wring[slot, part_, :, c : c + step], preferred_element_type=F32)
                    acc[e, :, part_ * ff + c : part_ * ff + c + step] += got

            @pl.when(i + WR < experts * kn)
            def _():
                for copy in w_copies(i + WR):
                    copy.start()

            @pl.when(k == kn - 1)
            def _():
                for c in range(0, ff, 256):
                    g = acc[e, :, c : c + 256]
                    u = acc[e, :, ff + c : ff + c + 256]
                    hid[e, :, c : c + 256] = (g * lax.logistic(g) * u).astype(BF16)

            return 0

        lax.fori_loop(0, experts, one, 0)

    def gather_step(t, _):
        @pl.when(t < kn)
        def _():
            to_x(t).wait_recv()
            x_to_core(t).start()
            x_to_y(t).start()
            to_y(t).wait_recv()
            y_to_core(t).start()
            y_to_x(t).start()

        @pl.when(t + 2 < kn)
        def _():
            first_hop(t + 2)

        @pl.when((t >= 1) & (t < kn + 1))
        def _():
            x_to_y(t - 1).wait_recv()
            y_to_x(t - 1).wait_recv()
            xy_to_core(t - 1).start()

        @pl.when((t >= 2) & (t < kn + 2))
        def _():
            k = t - 2
            to_core(k).wait_recv()
            x_to_core(k).wait_recv()
            y_to_core(k).wait_recv()
            xy_to_core(k).wait_recv()

            @pl.when(k == kn - 1)
            def _():
                for i in range(DR):
                    d_copy(i).start()

            project(k)

        return 0

    lax.fori_loop(0, kn + 2, gather_step, 0)

    def to_part(n):
        return remote(psend.at[n % 2], prec.at[n], p_ss.at[n], p_rs.at[n], CORE)

    def hop1_x(n):
        return remote(s1x.at[n % 2], r1x.at[n], h1_ss.at[0, n], h1_rs.at[0, n], X)

    def hop1_y(n):
        return remote(s1y.at[n % 2], r1y.at[n], h1_ss.at[1, n], h1_rs.at[1, n], Y)

    def hop2_x(n):
        return remote(s2x.at[n % 2], r2x.at[n], h2_ss.at[0, n], h2_rs.at[0, n], X)

    def hop2_y(n):
        return remote(s2y.at[n % 2], r2y.at[n], h2_ss.at[1, n], h2_rs.at[1, n], Y)

    top, low = slice(0, half), slice(half, tokens)

    def reduce_step(t, _):
        @pl.when((t >= 1) & (t < nn + 1))
        def _():
            n = t - 1
            to_part(n).wait_recv()

            @pl.when(n >= 2)
            def _():
                hop1_x(n - 2).wait_send()
                hop1_y(n - 2).wait_send()

            for q in range(4):
                part[n % 2, q] += prec[n, q].astype(F32)
            s1x[n % 2, 0] = part[n % 2, 2, top].astype(BF16)
            s1x[n % 2, 1] = part[n % 2, 3, top].astype(BF16)
            hop1_x(n).start()
            s1y[n % 2, 0] = part[n % 2, 1, low].astype(BF16)
            s1y[n % 2, 1] = part[n % 2, 3, low].astype(BF16)
            hop1_y(n).start()
            keep[n % 4, 0, top] = part[n % 2, 1, top]
            keep[n % 4, 0, low] = part[n % 2, 2, low]
            keep[n % 4, 1] = part[n % 2, 0]

        @pl.when((t >= 2) & (t < nn + 2))
        def _():
            n = t - 2

            @pl.when(n >= 2)
            def _():
                hop2_x(n - 2).wait_send()
                hop2_y(n - 2).wait_send()

            hop1_x(n).wait_recv()
            s2y[n % 2] = (keep[n % 4, 0, top] + r1x[n, 1].astype(F32)).astype(BF16)
            hop2_y(n).start()
            hop1_y(n).wait_recv()
            s2x[n % 2] = (keep[n % 4, 0, low] + r1y[n, 1].astype(F32)).astype(BF16)
            hop2_x(n).start()

        @pl.when((t >= 3) & (t < nn + 3))
        def _():
            n = t - 3
            at = pl.ds(pl.multiple_of(n * nc, nc), nc)
            hop2_y(n).wait_recv()
            o_ref[top, at] = (
                keep[n % 4, 1, top] + r1x[n, 0].astype(F32) + r2y[n].astype(F32)
            ).astype(BF16)
            hop2_x(n).wait_recv()
            o_ref[low, at] = (
                keep[n % 4, 1, low] + r1y[n, 0].astype(F32) + r2x[n].astype(F32)
            ).astype(BF16)

        @pl.when(t < nn)
        def _():
            n = t

            def two(q, _):
                got = []
                for b in range(2):
                    i = n * experts + 2 * q + b
                    d_copy(i).wait()
                    got.append(
                        jnp.dot(hid[2 * q + b], dring[i % DR], preferred_element_type=F32).reshape(8, slots, nc)
                    )
                outb[q] = jnp.concatenate(got, axis=1).astype(BF16)
                for b in range(2):
                    i = n * experts + 2 * q + b

                    @pl.when(i + DR < experts * nn)
                    def _():
                        d_copy(i + DR).start()

                return 0

            lax.fori_loop(0, experts // 2, two, 0)

            @pl.when(n >= 2)
            def _():
                to_part(n - 2).wait_send()

            for r in (1, 3, 5, 7, 0, 2, 4, 6):
                sums = jnp.dot(comb[r], outb[:, r].reshape(rows, nc), preferred_element_type=F32)
                if r % 2:
                    psend[n % 2, r // 2] = sums.astype(BF16)
                else:
                    part[n % 2, r // 2] = sums
                if r == 7:
                    to_part(n).start()

        return 0

    lax.fori_loop(0, nn + 3, reduce_step, 0)

    def drain(k, _):
        for copy in exchange:
            copy(k).wait_send()
        return 0

    lax.fori_loop(0, kn, drain, 0)
    for n in (nn - 2, nn - 1):
        for copy in (to_part, hop1_x, hop1_y, hop2_x, hop2_y):
            copy(n).wait_send()


def solution(mesh):
    def local(x, expert, slot, gate, w_gate, w_up, w_down):
        x = x.reshape(x.shape[-2:])
        tokens, d = x.shape
        top = expert.shape[-1]
        experts, _, ff = w_gate.shape
        total = experts * mesh.shape["ep"]
        slots = 5 * tokens * top // (4 * total)
        kc = nc = 256
        kn, nn = d // kc, d // nc
        rows, half = experts * slots, tokens // 2
        code = jnp.where(slot < slots, expert * slots + slot, -1).astype(F32)
        meta = jnp.concatenate([code, gate.astype(BF16).astype(F32)], axis=-1).reshape(tokens, 2 * top).T
        dma = pltpu.SemaphoreType.DMA
        any_ = pl.BlockSpec(memory_space=pl.ANY)
        y = pl.pallas_call(
            functools.partial(kernel, (tokens, d, ff, experts, slots, kc, nc)),
            out_shape=jax.ShapeDtypeStruct((tokens, d), BF16),
            in_specs=[any_] * 5,
            out_specs=pl.BlockSpec(memory_space=pltpu.VMEM),
            scratch_shapes=[
                pltpu.VMEM((8, 2 * top, tokens), F32),
                pltpu.VMEM((8, kn, tokens, kc), BF16),
                pltpu.VMEM((experts, 8 * slots, 2 * ff), F32),
                pltpu.VMEM((experts, 8 * slots, ff), BF16),
                pltpu.VMEM((experts, 8 * slots, kc), BF16),
                pltpu.VMEM((WR, 2, kc, ff), BF16),
                pltpu.VMEM((DR, ff, nc), BF16),
                pltpu.VMEM((8, rows, tokens), BF16),
                pltpu.VMEM((8, tokens, rows), BF16),
                pltpu.VMEM((experts // 2, 8, 2 * slots, nc), BF16),
                pltpu.VMEM((2, 4, tokens, nc), F32),
                pltpu.VMEM((2, 4, tokens, nc), BF16),
                pltpu.VMEM((nn, 4, tokens, nc), BF16),
                pltpu.VMEM((4, 2, tokens, nc), F32),
                pltpu.VMEM((2, 2, half, nc), BF16),
                pltpu.VMEM((2, 2, half, nc), BF16),
                pltpu.VMEM((nn, 2, half, nc), BF16),
                pltpu.VMEM((nn, 2, half, nc), BF16),
                pltpu.VMEM((2, half, nc), BF16),
                pltpu.VMEM((2, half, nc), BF16),
                pltpu.VMEM((nn, half, nc), BF16),
                pltpu.VMEM((nn, half, nc), BF16),
                dma((8,)), dma((8,)),
                dma((kn + 1,)),
                dma((8, kn)), dma((8, kn)),
                dma((WR, 2)), dma((DR,)),
                dma((nn,)), dma((nn,)),
                dma((2, nn)), dma((2, nn)), dma((2, nn)), dma((2, nn)),
            ],
            compiler_params=pltpu.CompilerParams(
                collective_id=0, has_side_effects=True, vmem_limit_bytes=67_000_000
            ),
        )(meta, x, w_gate, w_up, w_down)
        return y[None, None]

    tok = P("dp", "ep", None, None)
    ws = P("ep", None, None)
    return jax.shard_map(
        local, mesh=mesh, in_specs=(tok, tok, tok, tok, ws, ws, ws), out_specs=tok, check_vma=False
    )
```

time: 338 us -> 127 us (0.38)
  Pallas kernels: 0 us -> 122 us
  blocking collectives: 120 us -> 0 us
  waiting for transfers between devices: 105 us -> 0 us
  matrix products: 84.6 us -> 0 us
  local copies, waits for them, and re-layouts: 23.2 us -> 2.3 us
  starting transfers between devices: 4.23 us -> 0 us
    pallas_call x0 -> x1, Pallas kernels: none -> 122 us  [local(): pl.pallas_call(functools.partial(kernel, (tokens, d, ff, experts, slots,...]
    another operation x1 -> x0, blocking collectives: 120 us -> none  [placed(): return lax.with_sharding_constraint(v, NamedSharding(mesh, P(*spec)))]
    another operation x1 -> x0, waiting for transfers between devices: 105 us -> none  [placed(): return lax.with_sharding_constraint(v, NamedSharding(mesh, P(*spec)))]
    dot_general x7 -> x0, matrix products: 84.6 us -> none  [einsum(): return jnp.einsum(form, a.astype(jnp.float32), b.astype(jnp.float32))]
    convert_element_type x3 -> x0, local copies, waits for them, and re-layouts: 11.4 us -> none  [the longest x1 5.62 us: step(): einsum('abtke,abtkc->abtec', weighted, to_slot).astype(jnp.bfloat16)]
    another operation x1 -> x0, local copies, waits for them, and re-layouts: 10.1 us -> none  [placed(): return lax.with_sharding_constraint(v, NamedSharding(mesh, P(*spec)))]
    another operation x1 -> x0, starting transfers between devices: 4.23 us -> none  [placed(): return lax.with_sharding_constraint(v, NamedSharding(mesh, P(*spec)))]
  transfers between devices with their start and end apart: 1 -> 0, of which waited for: 1 -> 0; matrix products, arithmetic and copies ran while one was open for 3% -> 0% of each run, Pallas kernels for 0% -> 0%
where the time goes in v1:
time: 127 us
  Pallas kernels  122 us (96%)
  local copies, waits for them, and re-layouts  2.3 us (2%)
  other arithmetic  2.02 us (2%)
    pallas_call x1, Pallas kernels, local(): pl.pallas_call(functools.partial(kernel, (tokens, d, ff, experts, slots,...  122 us

profile of v1, /device:TPU:0, one launch (start us, length us, event | category | flops | bytes accessed | tf_op | source)
XLA Modules:
  0.0 126.7 jit_solution(12200863087656972091)
XLA Ops:
  0.0 0.7 select_convert_fusion
  0.7 0.7 convert_convert_fusion
  1.4 0.6 maximum_bitcast_fusion.meta_ref
  2.0 122.3 %shard_map.73 = bf16[256,2048]{1,0:T(8,128)(2,1)} custom-call(f32[16,256]{1,0:T(8,128)} %maximum_bitcast_fusion.meta_ref, bf16[256,2048]{1,0:T(8,128)(2,1)} %bitcast.7, bf16[8,2048,1024]{2,1,0:T(8,128)(2,1)} %wg_ref.1, bf16[8,2048,1024]{2,1,0:T(8,128)(2,1)} %wu_ref.1, bf16[8,1024,2048]{2,1,0:T(8,128)(2,1)} %wd_ref.1), custom_call_target="tpu_custom_call" | custom-call | tf_op jit(solution)/shard_map/pallas_call | solution.py:355
  124.3 2.3 %copy.9 = bf16[1,1,256,2048]{3,2,1,0:T(8,128)(2,1)} copy(bf16[1,1,256,2048]{3,2,1,0:T(8,128)(2,1)} %bitcast.6) | data formatting | bytes 2097152

commit v2 on v1

v2 whole, which is shorter than its diff:
```python
import functools

import jax
import jax.numpy as jnp
from jax import lax
from jax.experimental import pallas as pl
from jax.experimental.pallas import tpu as pltpu
from jax.sharding import PartitionSpec as P

MESH = pl.DeviceIdType.MESH
F32, BF16 = jnp.float32, jnp.bfloat16

CORE, Y, X = 1, 2, 4
WR, DR = 12, 8
L1, L2, L3 = 1, 3, 4
GROUP = 4


def kernel(
    cfg, expert_ref, slot_ref, gate_ref, x_ref, wg_ref, wu_ref, wd_ref, o_ref,
    meta, gates, xall, acc, hid, z, wring, dring, disp, comb, prec, r1x, r1y, r2x, r2y,
    meta_ss, meta_rs, load_s, ag_ss, ag_rs, wsem, dsem, p_ss, p_rs, h1_ss, h1_rs, h2_ss, h2_rs,
):
    tokens, d, ff, experts, slots, kc, nc = cfg
    rows = experts * slots
    kn, nn = d // kc, d // nc
    half = tokens // 2
    wide = 2 * slots
    dp, me = lax.axis_index("dp"), lax.axis_index("ep")

    def dev(mask):
        to = me
        for bit in (CORE, Y, X):
            if mask & bit:
                to = to + bit - 2 * bit * ((me // bit) % 2)
        return (dp, to)

    def remote(src, dst, ss, rs, mask):
        return pltpu.make_async_remote_copy(
            src_ref=src, dst_ref=dst, send_sem=ss, recv_sem=rs, device_id=dev(mask), device_id_type=MESH
        )

    def w_copies(i):
        e, k, slot = i % experts, i // experts, i % WR
        at = pl.ds(pl.multiple_of(k * kc, kc), kc)
        return (
            pltpu.make_async_copy(wg_ref.at[e, at], wring.at[slot, 0], wsem.at[slot, 0]),
            pltpu.make_async_copy(wu_ref.at[e, at], wring.at[slot, 1], wsem.at[slot, 1]),
        )

    def d_copy(i):
        e, n, slot = i % experts, i // experts, i % DR
        at = pl.ds(pl.multiple_of(n * nc, nc), nc)
        return pltpu.make_async_copy(wd_ref.at[e, :, at], dring.at[slot], dsem.at[slot])

    def to_x(k):
        return remote(xall.at[0, k], xall.at[X, k], ag_ss.at[0, k], ag_rs.at[0, k], X)

    def to_y(k):
        return remote(xall.at[0, k], xall.at[Y, k], ag_ss.at[1, k], ag_rs.at[1, k], Y)

    def to_core(k):
        return remote(xall.at[0, k], xall.at[CORE, k], ag_ss.at[2, k], ag_rs.at[2, k], CORE)

    def x_to_core(k):
        return remote(xall.at[X, k], xall.at[X | CORE, k], ag_ss.at[3, k], ag_rs.at[3, k], CORE)

    def y_to_core(k):
        return remote(xall.at[Y, k], xall.at[Y | CORE, k], ag_ss.at[4, k], ag_rs.at[4, k], CORE)

    def x_to_y(k):
        at = pl.ds(0, half)
        return remote(xall.at[X, k, at], xall.at[X | Y, k, at], ag_ss.at[5, k], ag_rs.at[5, k], Y)

    def y_to_x(k):
        at = pl.ds(half, half)
        return remote(xall.at[Y, k, at], xall.at[X | Y, k, at], ag_ss.at[6, k], ag_rs.at[6, k], X)

    def xy_to_core(k):
        return remote(xall.at[X | Y, k], xall.at[7, k], ag_ss.at[7, k], ag_rs.at[7, k], CORE)

    exchange = (to_x, to_y, to_core, x_to_core, y_to_core, x_to_y, y_to_x, xy_to_core)

    def own(k):
        at = pl.ds(pl.multiple_of(k * kc, kc), kc)
        return pltpu.make_async_copy(x_ref.at[:, at], xall.at[0, k], load_s.at[k])

    for k in range(kn):
        own(k).start()
    loads = [
        pltpu.make_async_copy(expert_ref, meta.at[0, 0], load_s.at[kn]),
        pltpu.make_async_copy(slot_ref, meta.at[0, 1], load_s.at[kn + 1]),
        pltpu.make_async_copy(gate_ref, gates.at[0], load_s.at[kn + 2]),
    ]
    for copy in loads:
        copy.start()
    for i in range(WR):
        for copy in w_copies(i):
            copy.start()

    barrier = pltpu.get_barrier_semaphore()
    for mask in range(1, 8):
        pl.semaphore_signal(barrier, inc=1, device_id=dev(mask), device_id_type=MESH)
    for copy in loads:
        copy.wait()
    pl.semaphore_wait(barrier, 7)

    metas = []
    for mask in range(1, 8):
        metas.append(remote(meta.at[0], meta.at[mask], meta_ss.at[0, mask], meta_rs.at[0, mask], mask))
        metas.append(remote(gates.at[0], gates.at[mask], meta_ss.at[1, mask], meta_rs.at[1, mask], mask))
    for copy in metas:
        copy.start()

    def first_hop(k):
        own(k).wait()
        to_x(k).start()
        to_y(k).start()
        to_core(k).start()

    first_hop(0)
    first_hop(1)

    def clear(e, _):
        acc[e] = jnp.zeros(acc.shape[1:], F32)
        return 0

    lax.fori_loop(0, experts, clear, 0)

    for copy in metas:
        copy.wait()

    def tables(r, _):
        row = lax.broadcasted_iota(jnp.int32, (rows, tokens), 0)
        slot = meta[r, 1]
        code = jnp.where(slot < slots, meta[r, 0] * slots + slot - me * rows, -1)
        gate = gates[r].astype(BF16).astype(F32)
        hit = jnp.zeros((rows, tokens), F32)
        weight = jnp.zeros((rows, tokens), F32)
        for j in range(8):
            same = code[j : j + 1] == row
            hit = jnp.where(same, 1.0, hit)
            weight = jnp.where(same, gate[j : j + 1], weight)
        disp[r] = hit.astype(BF16)
        comb[r] = jnp.transpose(weight).astype(BF16)
        return 0

    lax.fori_loop(0, 8, tables, 0)

    def place(k):
        for copy in (to_core, x_to_core, y_to_core, xy_to_core):
            copy(k).wait_recv()
        for pair in range(4):
            z0 = jnp.dot(disp[2 * pair], xall[2 * pair, k], preferred_element_type=F32)
            z1 = jnp.dot(disp[2 * pair + 1], xall[2 * pair + 1, k], preferred_element_type=F32)
            both = jnp.concatenate([z0.reshape(experts, slots, kc), z1.reshape(experts, slots, kc)], axis=1)
            z[:, pair * wide : (pair + 1) * wide, :] = both.astype(BF16)

    def project(k, run, last):
        first = k * experts + run * GROUP
        for b in range(GROUP):
            for copy in w_copies(first + b):
                copy.wait()
        step = 256
        for b in range(GROUP):
            e, ring = run * GROUP + b, (first + b) % WR
            lhs = z[e]
            for c in range(0, ff, step):
                at, up = slice(c, c + step), slice(ff + c, ff + c + step)
                g = acc[e, :, at] + jnp.dot(lhs, wring[ring, 0, :, at], preferred_element_type=F32)
                u = acc[e, :, up] + jnp.dot(lhs, wring[ring, 1, :, at], preferred_element_type=F32)
                if last:
                    hid[e, :, at] = (g * lax.logistic(g) * u).astype(BF16)
                else:
                    acc[e, :, at] = g
                    acc[e, :, up] = u
        if not last:
            for b in range(GROUP):

                @pl.when(first + b + WR < experts * kn)
                def _():
                    for copy in w_copies(first + b + WR):
                        copy.start()

    def gather_step(t, _):
        @pl.when(t < kn)
        def _():
            to_x(t).wait_recv()
            x_to_core(t).start()
            x_to_y(t).start()
            to_y(t).wait_recv()
            y_to_core(t).start()
            y_to_x(t).start()

        @pl.when(t + 2 < kn)
        def _():
            first_hop(t + 2)

        @pl.when(t >= 2)
        def _():
            project(t - 2, 1, False)

        @pl.when(t >= 1)
        def _():
            x_to_y(t - 1).wait_recv()
            y_to_x(t - 1).wait_recv()
            xy_to_core(t - 1).start()

        @pl.when((t >= 1) & (t < kn))
        def _():
            place(t - 1)
            project(t - 1, 0, False)

        return 0

    lax.fori_loop(0, kn + 1, gather_step, 0)
    for i in range(DR):
        d_copy(i).start()
    place(kn - 1)

    def last_step(run, _):
        project(kn - 1, run, True)
        return 0

    lax.fori_loop(0, experts // GROUP, last_step, 0)

    def drain(k, _):
        for copy in exchange:
            copy(k).wait_send()
        return 0

    lax.fori_loop(0, kn, drain, 0)

    top, low = pl.ds(0, half), pl.ds(half, half)

    def to_part(n, q):
        return remote(xall.at[2 * q + 1, n], prec.at[n, q], p_ss.at[n, q], p_rs.at[n, q], CORE)

    def hop1_x(n):
        return remote(xall.at[0, n], r1x.at[n], h1_ss.at[0, n], h1_rs.at[0, n], X)

    def hop1_y(n):
        return remote(xall.at[X, n], r1y.at[n], h1_ss.at[1, n], h1_rs.at[1, n], Y)

    def hop2_x(n):
        return remote(xall.at[Y, n, low], r2x.at[n], h2_ss.at[0, n], h2_rs.at[0, n], X)

    def hop2_y(n):
        return remote(xall.at[Y, n, top], r2y.at[n], h2_ss.at[1, n], h2_rs.at[1, n], Y)

    def col(q):
        return slice(q * nc, (q + 1) * nc)

    def last_projection(n):
        def run(g, _):
            first = n * experts + 4 * g
            for b in range(4):
                d_copy(first + b).wait()
            for a in range(2):
                got = [
                    jnp.dot(
                        hid[4 * g + 2 * a + b], dring[(first + 2 * a + b) % DR], preferred_element_type=F32
                    ).reshape(8, slots, nc)
                    for b in range(2)
                ]
                both = jnp.concatenate(got, axis=1).astype(BF16)
                for b in range(2):
                    z[4 * g + 2 * a + b] = both[4 * b : 4 * b + 4].reshape(8 * slots, nc)
            for b in range(4):

                @pl.when(first + b + DR < experts * nn)
                def _():
                    d_copy(first + b + DR).start()

            return 0

        lax.fori_loop(0, experts // 4, run, 0)
        for r in (1, 3, 5, 7, 0, 2, 4, 6):
            at = slice(r % 4 * wide, (r % 4 + 1) * wide)
            mine = jnp.concatenate([z[2 * q + r // 4, at] for q in range(experts // 2)], axis=0)
            sums = jnp.dot(comb[r], mine, preferred_element_type=F32)
            if r % 2:
                xall[r, n] = sums.astype(BF16)
                to_part(n, r // 2).start()
            else:
                acc[n, :tokens, col(r // 2)] = sums

    def sum_cores(n):
        for q in (3, 2, 1, 0):
            to_part(n, q).wait_recv()
            both = acc[n, :tokens, col(q)] + prec[n, q].astype(F32)
            acc[n, :tokens, col(q)] = both
            both = both.astype(BF16)
            if q == 3:
                xall[0, n, low] = both[:half]
                xall[X, n, low] = both[half:]
            if q == 2:
                xall[0, n, top] = both[:half]
                hop1_x(n).start()
            if q == 1:
                xall[X, n, top] = both[half:]
                hop1_y(n).start()

    def sum_first(n):
        hop1_x(n).wait_recv()
        xall[Y, n, top] = (acc[n, top, col(1)] + r1x[n, low].astype(F32)).astype(BF16)
        hop2_y(n).start()
        hop1_y(n).wait_recv()
        xall[Y, n, low] = (acc[n, low, col(2)] + r1y[n, low].astype(F32)).astype(BF16)
        hop2_x(n).start()

    def sum_second(n):
        at = pl.ds(pl.multiple_of(n * nc, nc), nc)
        hop2_y(n).wait_recv()
        o_ref[top, at] = (acc[n, top, col(0)] + r1x[n, top].astype(F32) + r2y[n].astype(F32)).astype(BF16)
        hop2_x(n).wait_recv()
        o_ref[low, at] = (acc[n, low, col(0)] + r1y[n, top].astype(F32) + r2x[n].astype(F32)).astype(BF16)

    def reduce_step(t, _):
        for lag, stage in ((L1, sum_cores), (L2, sum_first), (L3, sum_second), (0, last_projection)):

            @pl.when((t >= lag) & (t < nn + lag))
            def _():
                stage(t - lag)

        return 0

    lax.fori_loop(0, nn + L3, reduce_step, 0)

    def drain_sums(n, _):
        for q in range(4):
            to_part(n, q).wait_send()
        for copy in (hop1_x, hop1_y, hop2_x, hop2_y):
            copy(n).wait_send()
        return 0

    lax.fori_loop(0, nn, drain_sums, 0)


def solution(mesh):
    def local(x, expert, slot, gate, w_gate, w_up, w_down):
        x = x.reshape(x.shape[-2:])
        tokens, d = x.shape
        top = expert.shape[-1]
        experts, _, ff = w_gate.shape
        total = experts * mesh.shape["ep"]
        slots = 5 * tokens * top // (4 * total)
        kc = nc = 256
        kn, nn = d // kc, d // nc
        rows, half = experts * slots, tokens // 2
        expert, slot, gate = (v.reshape(tokens, top).T for v in (expert, slot, gate))
        dma = pltpu.SemaphoreType.DMA
        any_ = pl.BlockSpec(memory_space=pl.ANY)
        y = pl.pallas_call(
            functools.partial(kernel, (tokens, d, ff, experts, slots, kc, nc)),
            out_shape=jax.ShapeDtypeStruct((tokens, d), BF16),
            in_specs=[any_] * 7,
            out_specs=pl.BlockSpec(memory_space=pltpu.VMEM),
            scratch_shapes=[
                pltpu.VMEM((8, 2, top, tokens), jnp.int32),
                pltpu.VMEM((8, top, tokens), F32),
                pltpu.VMEM((8, kn, tokens, kc), BF16),
                pltpu.VMEM((experts, 8 * slots, 2 * ff), F32),
                pltpu.VMEM((experts, 8 * slots, ff), BF16),
                pltpu.VMEM((experts, 8 * slots, kc), BF16),
                pltpu.VMEM((WR, 2, kc, ff), BF16),
                pltpu.VMEM((DR, ff, nc), BF16),
                pltpu.VMEM((8, rows, tokens), BF16),
                pltpu.VMEM((8, tokens, rows), BF16),
                pltpu.VMEM((nn, 4, tokens, nc), BF16),
                pltpu.VMEM((nn, tokens, nc), BF16),
                pltpu.VMEM((nn, tokens, nc), BF16),
                pltpu.VMEM((nn, half, nc), BF16),
                pltpu.VMEM((nn, half, nc), BF16),
                dma((2, 8)), dma((2, 8)),
                dma((kn + 3,)),
                dma((8, kn)), dma((8, kn)),
                dma((WR, 2)), dma((DR,)),
                dma((nn, 4)), dma((nn, 4)),
                dma((2, nn)), dma((2, nn)), dma((2, nn)), dma((2, nn)),
            ],
            compiler_params=pltpu.CompilerParams(
                collective_id=0, has_side_effects=True, vmem_limit_bytes=67_000_000
            ),
        )(expert, slot, gate, x, w_gate, w_up, w_down)
        return y[None, None]

    tok = P("dp", "ep", None, None)
    ws = P("ep", None, None)
    return jax.shard_map(
        local, mesh=mesh, in_specs=(tok, tok, tok, tok, ws, ws, ws), out_specs=tok, check_vma=False
    )
```

time: 127 us -> 112 us (0.88)
  Pallas kernels: 122 us -> 110 us
  other arithmetic: 2.02 us -> 0 us
    pallas_call x1, Pallas kernels: 122 us -> 110 us  [local(): pl.pallas_call(functools.partial(kernel, (tokens, d, ff, experts, slots,...]
    convert_element_type x2 -> x0, other arithmetic: 1.42 us -> none  [the longest x1 0.72 us: local(): code = jnp.where(slot < slots, expert * slots + slot, -1).astype(F32)]
where the time goes in v2:
time: 112 us
  Pallas kernels  110 us (98%)
  local copies, waits for them, and re-layouts  2.3 us (2%)
    pallas_call x1, Pallas kernels, local(): pl.pallas_call(functools.partial(kernel, (tokens, d, ff, experts, slots,...  110 us
    unnamed x1, local copies, waits for them, and re-layouts  2.3 us

profile of v2, /device:TPU:0, one launch (start us, length us, event | category | flops | bytes accessed | tf_op | source)
XLA Modules:
  0.0 112.1 jit_solution(3568371130783322620)
XLA Ops:
  0.0 109.8 %shard_map.73 = bf16[256,2048]{1,0:T(8,128)(2,1)} custom-call(s32[8,256]{1,0:T(8,128)} %bitcast.13, s32[8,256]{1,0:T(8,128)} %bitcast.14, f32[8,256]{1,0:T(8,128)} %bitcast.15, bf16[256,2048]{1,0:T(8,128)(2,1)} %bitcast.12, bf16[8,2048,1024]{2,1,0:T(8,128)(2,1)} %wg_ref.1, bf16[8,2048,1024]{2,1,0:T(8,128)(2,1)} %wu_ref.1, bf16[8,1024,2048]{2,1,0:T(8,128)(2,1)} %wd_ref.1), custom_call_target="tpu_custom_call" | custom-call | tf_op jit(solution)/shard_map/pallas_call | solution.py:354
  109.8 2.3 %copy.9 = bf16[1,1,256,2048]{3,2,1,0:T(8,128)(2,1)} copy(bf16[1,1,256,2048]{3,2,1,0:T(8,128)(2,1)} %bitcast.11) | data formatting | bytes 2097152

commit v3 on v2

v3 whole, which is shorter than its diff:
```python
import functools

import jax
import jax.numpy as jnp
from jax import lax
from jax.experimental import pallas as pl
from jax.experimental.pallas import tpu as pltpu
from jax.sharding import PartitionSpec as P

MESH = pl.DeviceIdType.MESH
F32, BF16 = jnp.float32, jnp.bfloat16

CORE, Y, X = 1, 2, 4
WR, DR = 12, 8
L2, L3 = 2, 5
GROUP = 4


def kernel(
    cfg, expert_ref, slot_ref, gate_ref, x_ref, wg_ref, wu_ref, wd_ref, o_ref,
    raw, rawg, codes, gates, xall, acc, hid, z, wring, dring, disp, comb, prec, r1, r2,
    meta_ss, meta_rs, load_s, send_s, ag_rs, wsem, dsem, p_rs, h1_rs, h2_rs, out_s,
):
    tokens, d, ff, experts, slots, kc, nc = cfg
    rows = experts * slots
    kn, nn = d // kc, d // nc
    half = tokens // 2
    wide = 2 * slots
    dp, me = lax.axis_index("dp"), lax.axis_index("ep")

    def dev(mask):
        to = me
        for bit in (CORE, Y, X):
            if mask & bit:
                to = to + bit - 2 * bit * ((me // bit) % 2)
        return (dp, to)

    def remote(src, dst, ss, rs, mask):
        return pltpu.make_async_remote_copy(
            src_ref=src, dst_ref=dst, send_sem=ss, recv_sem=rs, device_id=dev(mask), device_id_type=MESH
        )

    def landed(ref, sem):
        pltpu.make_async_copy(ref, ref, sem).wait()

    def w_start(first):
        for b in range(GROUP):
            i = first + b
            e, k, ring = i % experts, i // experts, i % WR
            at = pl.ds(pl.multiple_of(k * kc, kc), kc)
            sem = wsem.at[first // GROUP % (WR // GROUP)]
            pltpu.make_async_copy(wg_ref.at[e, at], wring.at[ring, 0], sem).start()
            pltpu.make_async_copy(wu_ref.at[e, at], wring.at[ring, 1], sem).start()

    def w_wait(first):
        landed(wring.at[pl.ds(first % WR, GROUP)], wsem.at[first // GROUP % (WR // GROUP)])

    def d_start(first):
        for b in range(4):
            i = first + b
            e, n, ring = i % experts, i // experts, i % DR
            at = pl.ds(pl.multiple_of(n * nc, nc), nc)
            pltpu.make_async_copy(wd_ref.at[e, :, at], dring.at[ring], dsem.at[first // 4 % (DR // 4)]).start()

    def d_wait(first):
        landed(dring.at[pl.ds(first % DR, 4)], dsem.at[first // 4 % (DR // 4)])

    top, low = pl.ds(0, half), pl.ds(half, half)

    def exchange(kind, src, dst, k, mask, at=None):
        src, dst = xall.at[src, k], xall.at[dst, k]
        if at is not None:
            src, dst = src.at[at], dst.at[at]
        return remote(src, dst, send_s, ag_rs.at[kind, k], mask)

    def first_x(k):
        return exchange(0, 0, X, k, X, top)

    def first_y(k):
        return exchange(0, 0, Y, k, Y, low)

    def second_x(k):
        return exchange(1, 0, X, k, X, low)

    def second_y(k):
        return exchange(1, 0, Y, k, Y, top)

    def to_core(k):
        return exchange(2, 0, CORE, k, CORE)

    def x_to_core(k):
        return exchange(2, X, X | CORE, k, CORE)

    def y_to_core(k):
        return exchange(2, Y, Y | CORE, k, CORE)

    def x_to_y(k):
        return exchange(3, X, X | Y, k, Y, top)

    def y_to_x(k):
        return exchange(3, Y, X | Y, k, X, low)

    def xy_to_core(k):
        return exchange(2, X | Y, 7, k, CORE)

    def own_start(k):
        at = pl.ds(pl.multiple_of(k * kc, kc), kc)
        pltpu.make_async_copy(x_ref.at[:, at], xall.at[0, k], load_s.at[3 + min(k, 2)]).start()

    loads = [
        pltpu.make_async_copy(expert_ref, raw.at[0], load_s.at[0]),
        pltpu.make_async_copy(slot_ref, raw.at[1], load_s.at[1]),
        pltpu.make_async_copy(gate_ref, rawg, load_s.at[2]),
    ]
    for copy in loads:
        copy.start()
    for k in range(2):
        own_start(k)
    barrier = pltpu.get_barrier_semaphore()
    for mask in range(1, 8):
        pl.semaphore_signal(barrier, inc=1, device_id=dev(mask), device_id_type=MESH)
    for copy in loads:
        copy.wait()
    codes[0] = jnp.where(raw[1] < slots, raw[0] * slots + raw[1], -1)
    gates[0] = rawg[...].astype(BF16)
    pl.semaphore_wait(barrier, 7)

    def send_codes(mask):
        return remote(codes.at[0], codes.at[mask], meta_ss.at[0], meta_rs.at[0], mask)

    def send_gates(mask):
        return remote(gates.at[0], gates.at[mask], meta_ss.at[1], meta_rs.at[1], mask)

    def send_first(k):
        first_x(k).start()
        first_y(k).start()

    def send_second(k):
        second_x(k).start()
        second_y(k).start()
        to_core(k).start()

    for mask in (6, 7, 4, 5, 2, 3, 1):
        send_codes(mask).start()
    landed(xall.at[0, 0], load_s.at[3])
    send_first(0)
    for mask in (6, 7, 4, 5, 2, 3, 1):
        send_gates(mask).start()
    send_second(0)
    landed(xall.at[0, 1], load_s.at[4])
    send_first(1)
    for k in range(2, kn):
        own_start(k)
    for i in range(0, WR, GROUP):
        w_start(i)

    def clear(e, _):
        acc[e] = jnp.zeros(acc.shape[1:], F32)
        return 0

    lax.fori_loop(0, experts, clear, 0)

    def table(r, values):
        row = lax.broadcasted_iota(jnp.int32, (rows, tokens), 0)
        code = codes[r] - me * rows
        out = jnp.zeros((rows, tokens), F32)
        for j in range(8):
            out = jnp.where(code[j : j + 1] == row, 1.0 if values is None else values[j : j + 1], out)
        return out

    def dispatch_table(r, _):
        disp[r] = table(r, None).astype(BF16)
        return 0

    def combine_table(r, _):
        comb[r] = jnp.transpose(table(r, gates[r].astype(F32))).astype(BF16)
        return 0

    landed(codes.at[pl.ds(1, 7)], meta_rs.at[0])
    lax.fori_loop(0, 8, dispatch_table, 0)

    def place(k):
        landed(xall.at[pl.ds(0, 4), k], ag_rs.at[2, k])
        for pair in range(4):
            z0 = jnp.dot(disp[2 * pair], xall[2 * pair, k], preferred_element_type=F32)
            z1 = jnp.dot(disp[2 * pair + 1], xall[2 * pair + 1, k], preferred_element_type=F32)
            both = jnp.concatenate([z0.reshape(experts, slots, kc), z1.reshape(experts, slots, kc)], axis=1)
            z[:, pair * wide : (pair + 1) * wide, :] = both.astype(BF16)

    def project(k, run, last):
        first = k * experts + run * GROUP
        w_wait(first)
        step = 256 if last else 512
        for b in range(GROUP):
            e, ring = run * GROUP + b, (first + b) % WR
            lhs = z[e]
            for c in range(0, ff, step):
                at, up = slice(c, c + step), slice(ff + c, ff + c + step)
                g = acc[e, :, at] + jnp.dot(lhs, wring[ring, 0, :, at], preferred_element_type=F32)
                u = acc[e, :, up] + jnp.dot(lhs, wring[ring, 1, :, at], preferred_element_type=F32)
                if last:
                    hid[e, :, at] = (g * lax.logistic(g) * u).astype(BF16)
                else:
                    acc[e, :, at] = g
                    acc[e, :, up] = u
        if not last:

            @pl.when(first + WR < experts * kn)
            def _():
                w_start(first + WR)

    def pass_first(k):
        landed(xall.at[0, k], ag_rs.at[0, k])
        x_to_y(k).start()
        y_to_x(k).start()

        @pl.when(k + 1 < kn)
        def _():
            send_second(k + 1)

    def pass_second(k):
        landed(xall.at[0, k], ag_rs.at[1, k])
        x_to_core(k).start()
        y_to_core(k).start()

        @pl.when(k + 2 < kn)
        def _():
            send_first(k + 2)

    def pass_across(k):
        landed(xall.at[X | Y, k], ag_rs.at[3, k])
        xy_to_core(k).start()

    def gather_step(t, _):
        @pl.when(t < kn)
        def _():
            pass_first(t)

        @pl.when(t >= 2)
        def _():
            project(t - 2, 0, False)

        pass_across(t - 1)

        @pl.when(t >= 2)
        def _():
            project(t - 2, 1, False)

        @pl.when(t < kn)
        def _():
            pass_second(t)

        place(t - 1)
        return 0

    pass_first(0)
    landed(xall.at[0, pl.ds(2, kn - 2)], load_s.at[5])
    pass_second(0)
    landed(gates.at[pl.ds(1, 7)], meta_rs.at[1])
    lax.fori_loop(0, 8, combine_table, 0)
    lax.fori_loop(1, kn + 1, gather_step, 0)
    for i in range(0, DR, 4):
        d_start(i)

    def last_step(run, _):
        project(kn - 1, run, True)
        return 0

    lax.fori_loop(0, experts // GROUP, last_step, 0)

    landed(xall.at[pl.ds(0, 7)], send_s)
    landed(codes.at[pl.ds(1, 7)], meta_ss.at[0])
    landed(gates.at[pl.ds(1, 7)], meta_ss.at[1])

    def to_part(n, q):
        return remote(xall.at[2 * q + 1, n], prec.at[n, q], send_s, p_rs.at[n], CORE)

    def hop1_x(n):
        return remote(xall.at[0, n], r1.at[n, 0], send_s, h1_rs.at[n], X)

    def hop1_y(n):
        return remote(xall.at[X, n], r1.at[n, 1], send_s, h1_rs.at[n], Y)

    def hop2_x(n):
        return remote(xall.at[Y, n, low], r2.at[n, 0], send_s, h2_rs.at[n], X)

    def hop2_y(n):
        return remote(xall.at[Y, n, top], r2.at[n, 1], send_s, h2_rs.at[n], Y)

    def col(q):
        return slice(q * nc, (q + 1) * nc)

    def last_projection(g, n):
        first = n * experts + 4 * g
        d_wait(first)
        for a in range(2):
            got = [
                jnp.dot(
                    hid[4 * g + 2 * a + b], dring[(first + 2 * a + b) % DR], preferred_element_type=F32
                ).reshape(8, slots, nc)
                for b in range(2)
            ]
            both = jnp.concatenate(got, axis=1).astype(BF16)
            for b in range(2):
                z[4 * g + 2 * a + b] = both[4 * b : 4 * b + 4].reshape(8 * slots, nc)

        @pl.when(first + DR < experts * nn)
        def _():
            d_start(first + DR)

    def combine(n):
        def sums(r):
            at = slice(r % 4 * wide, (r % 4 + 1) * wide)
            mine = jnp.concatenate([z[2 * q + r // 4, at] for q in range(experts // 2)], axis=0)
            return jnp.dot(comb[r], mine, preferred_element_type=F32)

        for r in (7, 5, 3, 1):
            xall[r, n] = sums(r).astype(BF16)
        for r in (7, 5, 3, 1):
            to_part(n, r // 2).start()
        for r in (6, 4, 2, 0):
            acc[n, :tokens, col(r // 2)] = sums(r)

    def sum_cores(n):
        landed(prec.at[n], p_rs.at[n])
        for q in (3, 2, 1, 0):
            both = acc[n, :tokens, col(q)] + prec[n, q].astype(F32)
            acc[n, :tokens, col(q)] = both
            both = both.astype(BF16)
            if q == 3:
                xall[0, n, low] = both[:half]
                xall[X, n, low] = both[half:]
            if q == 2:
                xall[0, n, top] = both[:half]
                hop1_x(n).start()
            if q == 1:
                xall[X, n, top] = both[half:]
                hop1_y(n).start()

    def sum_first(n):
        landed(r1.at[n], h1_rs.at[n])
        xall[Y, n, top] = (acc[n, top, col(1)] + r1[n, 0, low].astype(F32)).astype(BF16)
        hop2_y(n).start()
        xall[Y, n, low] = (acc[n, low, col(2)] + r1[n, 1, low].astype(F32)).astype(BF16)
        hop2_x(n).start()

    def put(n):
        at = pl.ds(pl.multiple_of(n * nc, nc), nc)
        return pltpu.make_async_copy(prec.at[n, 0], o_ref.at[:, at], out_s)

    def sum_second(n):
        landed(r2.at[n], h2_rs.at[n])
        prec[n, 0, top] = (acc[n, top, col(0)] + r1[n, 0, top].astype(F32) + r2[n, 1].astype(F32)).astype(BF16)
        prec[n, 0, low] = (acc[n, low, col(0)] + r1[n, 1, top].astype(F32) + r2[n, 0].astype(F32)).astype(BF16)
        put(n).start()

    stages = (
        (0, functools.partial(last_projection, 0)), (1, sum_cores), (0, functools.partial(last_projection, 1)),
        (0, combine), (L2, sum_first), (L3, sum_second),
    )

    def reduce_step(t, _):
        for lag, stage in stages:

            @pl.when((t >= lag) & (t < nn + lag))
            def _():
                stage(t - lag)

        return 0

    lax.fori_loop(0, nn + L3, reduce_step, 0)

    landed(xall.at[pl.ds(0, 7)], send_s)
    landed(xall.at[0], out_s)


def solution(mesh):
    def local(x, expert, slot, gate, w_gate, w_up, w_down):
        x = x.reshape(x.shape[-2:])
        tokens, d = x.shape
        top = expert.shape[-1]
        experts, _, ff = w_gate.shape
        total = experts * mesh.shape["ep"]
        slots = 5 * tokens * top // (4 * total)
        kc = nc = 256
        kn, nn = d // kc, d // nc
        rows, half = experts * slots, tokens // 2
        expert, slot, gate = (v.reshape(tokens, top).T for v in (expert, slot, gate))
        dma = pltpu.SemaphoreType.DMA
        any_ = pl.BlockSpec(memory_space=pl.ANY)
        y = pl.pallas_call(
            functools.partial(kernel, (tokens, d, ff, experts, slots, kc, nc)),
            out_shape=jax.ShapeDtypeStruct((tokens, d), BF16),
            in_specs=[any_] * 7,
            out_specs=any_,
            scratch_shapes=[
                pltpu.VMEM((2, top, tokens), jnp.int32),
                pltpu.VMEM((top, tokens), F32),
                pltpu.VMEM((8, top, tokens), jnp.int32),
                pltpu.VMEM((8, top, tokens), BF16),
                pltpu.VMEM((8, kn, tokens, kc), BF16),
                pltpu.VMEM((experts, 8 * slots, 2 * ff), F32),
                pltpu.VMEM((experts, 8 * slots, ff), BF16),
                pltpu.VMEM((experts, 8 * slots, kc), BF16),
                pltpu.VMEM((WR, 2, kc, ff), BF16),
                pltpu.VMEM((DR, ff, nc), BF16),
                pltpu.VMEM((8, rows, tokens), BF16),
                pltpu.VMEM((8, tokens, rows), BF16),
                pltpu.VMEM((nn, 4, tokens, nc), BF16),
                pltpu.VMEM((nn, 2, tokens, nc), BF16),
                pltpu.VMEM((nn, 2, half, nc), BF16),
                dma((2,)), dma((2,)),
                dma((6,)),
                dma,
                dma((4, kn)),
                dma((WR // GROUP,)), dma((DR // 4,)),
                dma((nn,)), dma((nn,)), dma((nn,)),
                dma,
            ],
            compiler_params=pltpu.CompilerParams(
                collective_id=0, has_side_effects=True, vmem_limit_bytes=67_000_000
            ),
        )(expert, slot, gate, x, w_gate, w_up, w_down)
        return y[None, None]

    tok = P("dp", "ep", None, None)
    ws = P("ep", None, None)
    return jax.shard_map(
        local, mesh=mesh, in_specs=(tok, tok, tok, tok, ws, ws, ws), out_specs=tok, check_vma=False
    )
```

time: 112 us -> 92.6 us (0.83)
  Pallas kernels: 110 us -> 90.2 us
    pallas_call x1, Pallas kernels: 110 us -> 90.2 us  [local(): pl.pallas_call(functools.partial(kernel, (tokens, d, ff, experts, slots,...]
where the time goes in v3:
time: 92.6 us; the launch traced here: 92.5 us
  Pallas kernels  90.2 us (97%)
  local copies, waits for them, and re-layouts  2.3 us (2%)
    pallas_call x1, Pallas kernels, local(): pl.pallas_call(functools.partial(kernel, (tokens, d, ff, experts, slots,...  90.2 us
    unnamed x1, local copies, waits for them, and re-layouts  2.3 us

profile of v3, /device:TPU:0, one launch (start us, length us, event | category | flops | bytes accessed | tf_op | source)
XLA Modules:
  0.0 92.5 jit_solution(7247656213247465501)
XLA Ops:
  0.0 90.2 %shard_map.73 = bf16[256,2048]{1,0:T(8,128)(2,1)} custom-call(s32[8,256]{1,0:T(8,128)} %bitcast.13, s32[8,256]{1,0:T(8,128)} %bitcast.14, f32[8,256]{1,0:T(8,128)} %bitcast.15, bf16[256,2048]{1,0:T(8,128)(2,1)} %bitcast.12, bf16[8,2048,1024]{2,1,0:T(8,128)(2,1)} %wg_ref.1, bf16[8,2048,1024]{2,1,0:T(8,128)(2,1)} %wu_ref.1, bf16[8,1024,2048]{2,1,0:T(8,128)(2,1)} %wd_ref.1), custom_call_target="tpu_custom_call" | custom-call | tf_op jit(solution)/shard_map/pallas_call | solution.py:391
  90.2 2.3 %copy.9 = bf16[1,1,256,2048]{3,2,1,0:T(8,128)(2,1)} copy(bf16[1,1,256,2048]{3,2,1,0:T(8,128)(2,1)} %bitcast.11) | data formatting | bytes 2097152

commit v4 on v3

--- a/solution.py
+++ b/solution.py
@@ -19,7 +19,7 @@
 def kernel(
     cfg, expert_ref, slot_ref, gate_ref, x_ref, wg_ref, wu_ref, wd_ref, o_ref,
     raw, rawg, codes, gates, xall, acc, hid, z, wring, dring, disp, comb, prec, r1, r2,
-    meta_ss, meta_rs, load_s, send_s, ag_rs, wsem, dsem, p_rs, h1_rs, h2_rs, out_s,
+    meta_ss, meta_rs, load_s, send_s, ag_rs, wsem, dsem, p_rs, h1_rs, h2_rs,
 ):
     tokens, d, ff, experts, slots, kc, nc = cfg
     rows = experts * slots
@@ -232,13 +232,13 @@
         xy_to_core(k).start()
 
     def gather_step(t, _):
+        @pl.when(t >= 2)
+        def _():
+            project(t - 2, 0, False)
+
         @pl.when(t < kn)
         def _():
             pass_first(t)
-
-        @pl.when(t >= 2)
-        def _():
-            project(t - 2, 0, False)
 
         pass_across(t - 1)
 
@@ -344,15 +344,11 @@
         xall[Y, n, low] = (acc[n, low, col(2)] + r1[n, 1, low].astype(F32)).astype(BF16)
         hop2_x(n).start()
 
-    def put(n):
+    def sum_second(n):
         at = pl.ds(pl.multiple_of(n * nc, nc), nc)
-        return pltpu.make_async_copy(prec.at[n, 0], o_ref.at[:, at], out_s)
-
-    def sum_second(n):
         landed(r2.at[n], h2_rs.at[n])
-        prec[n, 0, top] = (acc[n, top, col(0)] + r1[n, 0, top].astype(F32) + r2[n, 1].astype(F32)).astype(BF16)
-        prec[n, 0, low] = (acc[n, low, col(0)] + r1[n, 1, top].astype(F32) + r2[n, 0].astype(F32)).astype(BF16)
-        put(n).start()
+        o_ref[top, at] = (acc[n, top, col(0)] + r1[n, 0, top].astype(F32) + r2[n, 1].astype(F32)).astype(BF16)
+        o_ref[low, at] = (acc[n, low, col(0)] + r1[n, 1, top].astype(F32) + r2[n, 0].astype(F32)).astype(BF16)
 
     stages = (
         (0, functools.partial(last_projection, 0)), (1, sum_cores), (0, functools.partial(last_projection, 1)),
@@ -371,7 +367,6 @@
     lax.fori_loop(0, nn + L3, reduce_step, 0)
 
     landed(xall.at[pl.ds(0, 7)], send_s)
-    landed(xall.at[0], out_s)
 
 
 def solution(mesh):
@@ -390,9 +385,9 @@
         any_ = pl.BlockSpec(memory_space=pl.ANY)
         y = pl.pallas_call(
             functools.partial(kernel, (tokens, d, ff, experts, slots, kc, nc)),
-            out_shape=jax.ShapeDtypeStruct((tokens, d), BF16),
+            out_shape=pltpu.VMEM((tokens, d), BF16),
             in_specs=[any_] * 7,
-            out_specs=any_,
+            out_specs=pl.BlockSpec(memory_space=pltpu.VMEM),
             scratch_shapes=[
                 pltpu.VMEM((2, top, tokens), jnp.int32),
                 pltpu.VMEM((top, tokens), F32),
@@ -415,10 +410,9 @@
                 dma((4, kn)),
                 dma((WR // GROUP,)), dma((DR // 4,)),
                 dma((nn,)), dma((nn,)), dma((nn,)),
-                dma,
             ],
             compiler_params=pltpu.CompilerParams(
-                collective_id=0, has_side_effects=True, vmem_limit_bytes=67_000_000
+                collective_id=0, has_side_effects=True, vmem_limit_bytes=65_900_000
             ),
         )(expert, slot, gate, x, w_gate, w_up, w_down)
         return y[None, None]

time: 92.6 us -> 90.4 us (0.976)
  local copies, waits for them, and re-layouts: 2.3 us -> 0.97 us
    unnamed x1, local copies, waits for them, and re-layouts: 2.3 us -> 0.97 us
where the time goes in v4:
time: 90.4 us; the launch traced here: 90.3 us
  Pallas kernels  89.3 us (99%)
  local copies, waits for them, and re-layouts  0.97 us (1%)
    pallas_call x1, Pallas kernels, local(): pl.pallas_call(functools.partial(kernel, (tokens, d, ff, experts, slots,...  89.3 us

profile of v4, /device:TPU:0, one launch (start us, length us, event | category | flops | bytes accessed | tf_op | source)
XLA Modules:
  0.0 90.3 jit_solution(3493107282010765862)
XLA Ops:
  0.0 89.3 %shard_map.73 = bf16[256,2048]{1,0:T(8,128)(2,1)S(1)} custom-call(s32[8,256]{1,0:T(8,128)} %bitcast.13, s32[8,256]{1,0:T(8,128)} %bitcast.14, f32[8,256]{1,0:T(8,128)} %bitcast.15, bf16[256,2048]{1,0:T(8,128)(2,1)} %bitcast.12, bf16[8,2048,1024]{2,1,0:T(8,128)(2,1)} %wg_ref.1, bf16[8,2048,1024]{2,1,0:T(8,128)(2,1)} %wu_ref.1, bf16[8,1024,2048]{2,1,0:T(8,128)(2,1)} %wd_ref.1), custom_call_target="tpu_custom_call" | custom-call | tf_op jit(solution)/shard_map/pallas_call | solution.py:386
  89.3 1.0 %copy.9 = bf16[1,1,256,2048]{3,2,1,0:T(8,128)(2,1)} copy(bf16[1,1,256,2048]{3,2,1,0:T(8,128)(2,1)S(1)} %bitcast.11) | data formatting | bytes 2097152

commit v5 on v4

--- a/solution.py
+++ b/solution.py
@@ -121,7 +121,7 @@
         pl.semaphore_signal(barrier, inc=1, device_id=dev(mask), device_id_type=MESH)
     for copy in loads:
         copy.wait()
-    codes[0] = jnp.where(raw[1] < slots, raw[0] * slots + raw[1], -1)
+    codes[0] = jnp.where(raw[1] < slots, raw[0] * slots + raw[1], -1).astype(jnp.int16)
     gates[0] = rawg[...].astype(BF16)
     pl.semaphore_wait(barrier, 7)
 
@@ -162,7 +162,7 @@
 
     def table(r, values):
         row = lax.broadcasted_iota(jnp.int32, (rows, tokens), 0)
-        code = codes[r] - me * rows
+        code = codes[r].astype(jnp.int32) - me * rows
         out = jnp.zeros((rows, tokens), F32)
         for j in range(8):
             out = jnp.where(code[j : j + 1] == row, 1.0 if values is None else values[j : j + 1], out)
@@ -180,7 +180,6 @@
     lax.fori_loop(0, 8, dispatch_table, 0)
 
     def place(k):
-        landed(xall.at[pl.ds(0, 4), k], ag_rs.at[2, k])
         for pair in range(4):
             z0 = jnp.dot(disp[2 * pair], xall[2 * pair, k], preferred_element_type=F32)
             z1 = jnp.dot(disp[2 * pair + 1], xall[2 * pair + 1, k], preferred_element_type=F32)
@@ -189,7 +188,6 @@
 
     def project(k, run, last):
         first = k * experts + run * GROUP
-        w_wait(first)
         step = 256 if last else 512
         for b in range(GROUP):
             e, ring = run * GROUP + b, (first + b) % WR
@@ -231,26 +229,23 @@
         landed(xall.at[X | Y, k], ag_rs.at[3, k])
         xy_to_core(k).start()
 
+    def arrived(k):
+        landed(xall.at[pl.ds(0, 4), k], ag_rs.at[2, k])
+
     def gather_step(t, _):
+        pass_first(t)
+        pass_across(t - 1)
+
         @pl.when(t >= 2)
         def _():
-            project(t - 2, 0, False)
-
-        @pl.when(t < kn)
-        def _():
-            pass_first(t)
-
-        pass_across(t - 1)
-
-        @pl.when(t >= 2)
-        def _():
+            w_wait((t - 2) * experts + GROUP)
             project(t - 2, 1, False)
 
-        @pl.when(t < kn)
-        def _():
-            pass_second(t)
-
+        pass_second(t)
+        w_wait((t - 1) * experts)
+        arrived(t - 1)
         place(t - 1)
+        project(t - 1, 0, False)
         return 0
 
     pass_first(0)
@@ -258,15 +253,18 @@
     pass_second(0)
     landed(gates.at[pl.ds(1, 7)], meta_rs.at[1])
     lax.fori_loop(0, 8, combine_table, 0)
-    lax.fori_loop(1, kn + 1, gather_step, 0)
+    lax.fori_loop(1, kn, gather_step, 0)
+    pass_across(kn - 1)
+    w_wait((kn - 2) * experts + GROUP)
+    project(kn - 2, 1, False)
     for i in range(0, DR, 4):
         d_start(i)
-
-    def last_step(run, _):
+    w_wait((kn - 1) * experts)
+    w_wait((kn - 1) * experts + GROUP)
+    arrived(kn - 1)
+    place(kn - 1)
+    for run in range(experts // GROUP):
         project(kn - 1, run, True)
-        return 0
-
-    lax.fori_loop(0, experts // GROUP, last_step, 0)
 
     landed(xall.at[pl.ds(0, 7)], send_s)
     landed(codes.at[pl.ds(1, 7)], meta_ss.at[0])
@@ -292,7 +290,6 @@
 
     def last_projection(g, n):
         first = n * experts + 4 * g
-        d_wait(first)
         for a in range(2):
             got = [
                 jnp.dot(
@@ -307,6 +304,10 @@
         @pl.when(first + DR < experts * nn)
         def _():
             d_start(first + DR)
+
+    def last_run(g, n):
+        d_wait(n * experts + 4 * g)
+        last_projection(g, n)
 
     def combine(n):
         def sums(r):
@@ -351,7 +352,7 @@
         o_ref[low, at] = (acc[n, low, col(0)] + r1[n, 1, top].astype(F32) + r2[n, 0].astype(F32)).astype(BF16)
 
     stages = (
-        (0, functools.partial(last_projection, 0)), (1, sum_cores), (0, functools.partial(last_projection, 1)),
+        (0, functools.partial(last_run, 0)), (1, sum_cores), (0, functools.partial(last_run, 1)),
         (0, combine), (L2, sum_first), (L3, sum_second),
     )
 
@@ -391,7 +392,7 @@
             scratch_shapes=[
                 pltpu.VMEM((2, top, tokens), jnp.int32),
                 pltpu.VMEM((top, tokens), F32),
-                pltpu.VMEM((8, top, tokens), jnp.int32),
+                pltpu.VMEM((8, top, tokens), jnp.int16),
                 pltpu.VMEM((8, top, tokens), BF16),
                 pltpu.VMEM((8, kn, tokens, kc), BF16),
                 pltpu.VMEM((experts, 8 * slots, 2 * ff), F32),

time: 90.4 us -> 89.9 us (level)
  no operation moved by 1% of the time
where the time goes in v5:
time: 89.9 us; the launch traced here: 89.8 us
  Pallas kernels  88.8 us (99%)
  local copies, waits for them, and re-layouts  0.97 us (1%)
    pallas_call x1, Pallas kernels, local(): pl.pallas_call(functools.partial(kernel, (tokens, d, ff, experts, slots,...  88.8 us

profile of v5, /device:TPU:0, one launch (start us, length us, event | category | flops | bytes accessed | tf_op | source)
XLA Modules:
  0.0 89.8 jit_solution(3902887076688078307)
XLA Ops:
  0.0 88.8 %shard_map.73 = bf16[256,2048]{1,0:T(8,128)(2,1)S(1)} custom-call(s32[8,256]{1,0:T(8,128)} %bitcast.13, s32[8,256]{1,0:T(8,128)} %bitcast.14, f32[8,256]{1,0:T(8,128)} %bitcast.15, bf16[256,2048]{1,0:T(8,128)(2,1)} %bitcast.12, bf16[8,2048,1024]{2,1,0:T(8,128)(2,1)} %wg_ref.1, bf16[8,2048,1024]{2,1,0:T(8,128)(2,1)} %wu_ref.1, bf16[8,1024,2048]{2,1,0:T(8,128)(2,1)} %wd_ref.1), custom_call_target="tpu_custom_call" | custom-call | tf_op jit(solution)/shard_map/pallas_call | solution.py:387
  88.8 1.0 %copy.9 = bf16[1,1,256,2048]{3,2,1,0:T(8,128)(2,1)} copy(bf16[1,1,256,2048]{3,2,1,0:T(8,128)(2,1)S(1)} %bitcast.11) | data formatting | bytes 2097152

commit v6 on v5

--- a/solution.py
+++ b/solution.py
@@ -271,7 +271,7 @@
     landed(gates.at[pl.ds(1, 7)], meta_ss.at[1])
 
     def to_part(n, q):
-        return remote(xall.at[2 * q + 1, n], prec.at[n, q], send_s, p_rs.at[n], CORE)
+        return remote(xall.at[2 * q + 1, n], prec.at[n, q], send_s, p_rs.at[n % 2], CORE)
 
     def hop1_x(n):
         return remote(xall.at[0, n], r1.at[n, 0], send_s, h1_rs.at[n], X)
@@ -323,8 +323,8 @@
             acc[n, :tokens, col(r // 2)] = sums(r)
 
     def sum_cores(n):
-        landed(prec.at[n], p_rs.at[n])
-        for q in (3, 2, 1, 0):
+        landed(prec.at[n], p_rs.at[n % 2])
+        for q in (3, 1, 2, 0):
             both = acc[n, :tokens, col(q)] + prec[n, q].astype(F32)
             acc[n, :tokens, col(q)] = both
             both = both.astype(BF16)
@@ -410,7 +410,7 @@
                 dma,
                 dma((4, kn)),
                 dma((WR // GROUP,)), dma((DR // 4,)),
-                dma((nn,)), dma((nn,)), dma((nn,)),
+                dma((2,)), dma((nn,)), dma((nn,)),
             ],
             compiler_params=pltpu.CompilerParams(
                 collective_id=0, has_side_effects=True, vmem_limit_bytes=65_900_000

time: 89.9 us -> 89.8 us (level)
  no operation moved by 1% of the time
where the time goes in v6:
time: 89.8 us; the launch traced here: 89.7 us
  Pallas kernels  88.7 us (99%)
  local copies, waits for them, and re-layouts  0.97 us (1%)
    pallas_call x1, Pallas kernels, local(): pl.pallas_call(functools.partial(kernel, (tokens, d, ff, experts, slots,...  88.7 us

profile of v6, /device:TPU:0, one launch (start us, length us, event | category | flops | bytes accessed | tf_op | source)
XLA Modules:
  0.0 89.7 jit_solution(3486307963416962341)
XLA Ops:
  0.0 88.7 %shard_map.73 = bf16[256,2048]{1,0:T(8,128)(2,1)S(1)} custom-call(s32[8,256]{1,0:T(8,128)} %bitcast.13, s32[8,256]{1,0:T(8,128)} %bitcast.14, f32[8,256]{1,0:T(8,128)} %bitcast.15, bf16[256,2048]{1,0:T(8,128)(2,1)} %bitcast.12, bf16[8,2048,1024]{2,1,0:T(8,128)(2,1)} %wg_ref.1, bf16[8,2048,1024]{2,1,0:T(8,128)(2,1)} %wu_ref.1, bf16[8,1024,2048]{2,1,0:T(8,128)(2,1)} %wd_ref.1), custom_call_target="tpu_custom_call" | custom-call | tf_op jit(solution)/shard_map/pallas_call | solution.py:387
  88.7 1.0 %copy.9 = bf16[1,1,256,2048]{3,2,1,0:T(8,128)(2,1)} copy(bf16[1,1,256,2048]{3,2,1,0:T(8,128)(2,1)S(1)} %bitcast.11) | data formatting | bytes 2097152
